TPU v7x, 32 devices: a whole 2x2x4 slice. The times are simulated.
32 devices in a mesh: mem: 8 (over y, x, core), lat: 4 (over z).
Axes of the slice: x: 2, y: 2, z: 4, core: 2. Of those that a mesh axis runs over, the one named last changes fastest.
Arguments:
- state: float32 [8, 641, 8, 160], P('mem', None, 'lat'), may hold values from -6 to 6
- conv_kernel: float32 [25, 641], replicated, may hold values from -1.25 to 1.25
- norm_gain: float32 [641], replicated, may hold values from 0.5 to 1.5
- up_weight: bfloat16 [641, 1282], replicated, may hold values from -0.25 to 0.25
- down_weight: bfloat16 [1282, 641], replicated, may hold values from -0.15625 to 0.15625
- field_head_weight: bfloat16 [641, 72], replicated, may hold values from -0.25 to 0.25
- target: float32 [72, 8, 160], P(None, 'lat'), may hold values from -9 to 9
- field_weight: float32 [72], replicated, may hold values from 0.3 to 3
Outputs:
- loss: float32 [], replicated
- grad_kernel: float32 [25, 641], replicated
- grad_gain: float32 [641], replicated
- grad_up: float32 [641, 1282], replicated
- grad_down: float32 [1282, 641], replicated
- grad_head: float32 [641, 72], replicated
All inputs are finite; a program needn't handle non-finite values.
Results may differ from a plain program's by a relative error of at most 0.005.
The roundings to bfloat16 on the way count: a program that leaves them out, or rounds other values in their place, can miss the bound.
Values may be sent and summed in bfloat16 or wider, within the bound.
No kernel may reach another device: no remote copies, remote signals or barrier semaphores. Data moves between devices by JAX's collectives and lax.ppermute only.
A program may use at most 128 MiB of HBM per device.

v0:
```python
import math
import jax
import jax.numpy as jnp
from jax import lax
from jax.sharding import PartitionSpec as P

DELTA = 0.1
EPSILON = 1e-05


def extended(cells, sides, width):
    for axis, dim in sides:
        count = lax.axis_size(axis)
        ends = count - 1
        head = lax.slice_in_dim(cells, 0, width, axis=dim)
        tail = lax.slice_in_dim(cells, cells.shape[dim] - width, cells.shape[dim], axis=dim)
        cells = jnp.concatenate(
            [
                lax.ppermute(tail, axis, [(i, (i + 1) % count) for i in range(ends)]),
                cells,
                lax.ppermute(head, axis, [((i + 1) % count, i) for i in range(ends)]),
            ],
            axis=dim,
        )
    return cells


def softened_absolute(diff):
    return jnp.sqrt(diff * diff + DELTA * DELTA) - DELTA


def softened_derivative(diff):
    return diff / jnp.sqrt(diff * diff + DELTA * DELTA)


def gelu_parts(before_activation):
    cumul = 0.5 * (1.0 + jax.scipy.special.erf(before_activation / math.sqrt(2.0)))
    density = jnp.exp(-0.5 * before_activation * before_activation) / math.sqrt(2.0 * math.pi)
    return (before_activation * cumul, cumul + before_activation * density)


def leading_product(left, right):
    return lax.dot_general(
        left, right, (((0,), (0,)), ((), ())), preferred_element_type=jnp.float32
    )


def tail_dot(left, right):
    return lax.dot_general(
        left, right, (((1,), (1,)), ((), ())), preferred_element_type=jnp.float32
    )


def stencil(window, kernel, height):
    result = jnp.zeros((window.shape[0], height, window.shape[2]), jnp.float32)
    for col_off in range(5):
        shifted = jnp.roll(window, 2 - col_off, axis=2)
        for row_off in range(5):
            result = (
                result
                + kernel[row_off * 5 + col_off][:, None, None]
                * shifted[:, row_off : row_off + height]
            )
    return result


def kernel_grad(window, upstream, height):
    terms = [None] * 25
    for col_off in range(5):
        shifted = jnp.roll(window, 2 - col_off, axis=2)
        for row_off in range(5):
            terms[row_off * 5 + col_off] = jnp.sum(
                upstream * shifted[:, row_off : row_off + height], axis=(1, 2)
            )
    return jnp.stack(terms)


def forward_apply(field, window, kernel, gain, up_weight, down_weight, field_head_weight):
    height = field.shape[1]
    channels = field.shape[0]
    summed = (field + stencil(window, kernel, height)).reshape(channels, -1)
    center = summed - jnp.mean(summed, axis=0)
    inverse_norm = lax.rsqrt(jnp.mean(center * center, axis=0) + EPSILON)
    normalized_input = center * inverse_norm
    gain_scaled = (normalized_input * gain[:, None]).astype(jnp.bfloat16)
    before_activation = leading_product(up_weight, gain_scaled)
    activ, unused = gelu_parts(before_activation)
    hidden_activation = activ.astype(jnp.bfloat16)
    output = summed + leading_product(down_weight, hidden_activation)
    rounded_values = output.astype(jnp.bfloat16)
    member_prediction = leading_product(field_head_weight, rounded_values)
    return (
        member_prediction,
        (
            normalized_input,
            inverse_norm,
            gain_scaled,
            before_activation,
            hidden_activation,
            rounded_values,
        ),
    )


def backward(window, stored_residuals, cotangent, gain, up_weight, down_weight, field_head_weight):
    (
        normalized_input,
        inverse_norm,
        gain_scaled,
        before_activation,
        hidden_activation,
        rounded_values,
    ) = stored_residuals
    height = window.shape[1] - 4
    grad_head = tail_dot(rounded_values, cotangent)
    d_output = jnp.dot(field_head_weight, cotangent, preferred_element_type=jnp.float32)
    d_round = d_output.astype(jnp.bfloat16)
    grad_down = tail_dot(hidden_activation, d_round)
    d_hidden = jnp.dot(down_weight, d_round, preferred_element_type=jnp.float32)
    unused, slope = gelu_parts(before_activation)
    d_preact = (d_hidden * slope).astype(jnp.bfloat16)
    grad_up = tail_dot(gain_scaled, d_preact)
    d_scaled = jnp.dot(up_weight, d_preact, preferred_element_type=jnp.float32)
    grad_gain = jnp.sum(d_scaled * normalized_input, axis=1)
    d_normed = d_scaled * gain[:, None]
    d_summed = d_output + inverse_norm * (
        d_normed
        - jnp.mean(d_normed, axis=0)
        - normalized_input * jnp.mean(d_normed * normalized_input, axis=0)
    )
    upstream = d_summed.reshape(window.shape[0], height, window.shape[2])
    grad_kernel = kernel_grad(window, upstream, height)
    return (grad_kernel, grad_gain, grad_up, grad_down, grad_head)


def local(
    state, conv_kernel, norm_gain, up_weight, down_weight, field_head_weight, target, field_weight
):
    field = state[0]
    member_states = lax.axis_size("mem")
    height = field.shape[1]
    nlat = lax.axis_size("lat") * height
    width = field.shape[2]
    nfields = target.shape[0]
    window = extended(field, (("lat", 1),), 2)
    member_prediction, stored_residuals = forward_apply(
        field, window, conv_kernel, norm_gain, up_weight, down_weight, field_head_weight
    )
    grid_cell_values = member_prediction.shape[1]
    observed_target = target.reshape(nfields, grid_cell_values)
    row_float = (lax.axis_index("lat") * height + jnp.arange(height)).astype(jnp.float32)
    area_rows = jnp.cos(0.5 * math.pi * ((row_float + 0.5) / nlat - 1.0))
    area = jnp.repeat(area_rows, width)
    member_count = nlat * width * nfields
    scale_grad = 1.0 / (member_states * math.sqrt(member_count))
    pair_norm = 2.0 * member_states * (member_states - 1)
    block = grid_cell_values // member_states
    outgoing = member_prediction.reshape(1, nfields, member_states, block)
    gathered_members = lax.all_to_all(
        outgoing, "mem", split_axis=2, concat_axis=0, tiled=True
    ).reshape(member_states, nfields, block)
    mine = lax.axis_index("mem")
    truth_block = lax.dynamic_index_in_dim(
        observed_target.reshape(nfields, member_states, block), mine, 1, keepdims=False
    )
    area_block = lax.dynamic_index_in_dim(
        area.reshape(member_states, block), mine, 0, keepdims=False
    )
    differences = gathered_members[:, None] - gathered_members[None]
    ensemble_spread = (
        jnp.mean(softened_absolute(gathered_members - truth_block[None]), axis=0)
        - jnp.sum(softened_absolute(differences), axis=(0, 1)) / pair_norm
    )
    partial_value = jnp.sum(field_weight[:, None] * area_block[None, :] * ensemble_spread)
    loss = lax.psum(partial_value, ("mem", "lat")) / member_count
    pairwise_derivatives = jnp.sum(softened_derivative(differences), axis=1)
    member_cot = (
        field_weight[None, :, None]
        * area_block[None, None, :]
        * (
            softened_derivative(gathered_members - truth_block[None])
            - pairwise_derivatives / (member_states - 1)
        )
        * scale_grad
    )
    cot_rounded = member_cot.astype(jnp.bfloat16).reshape(member_states, nfields, 1, block)
    returned = lax.all_to_all(cot_rounded, "mem", split_axis=0, concat_axis=2, tiled=True)
    cotangent = returned.reshape(nfields, grid_cell_values)
    grads = backward(
        window, stored_residuals, cotangent, norm_gain, up_weight, down_weight, field_head_weight
    )
    totals = lax.psum((grads[0], grads[1], grads[2], grads[3], grads[4]), ("mem", "lat"))
    return (loss, totals[0], totals[1], totals[2], totals[3], totals[4])


def solution(mesh):
    return jax.shard_map(
        local,
        mesh=mesh,
        in_specs=(P("mem", None, "lat", None), P(), P(), P(), P(), P(), P(None, "lat", None), P()),
        out_specs=(P(), P(), P(), P(), P(), P()),
        check_vma=False,
    )
```

profile of v0, /device:TPU:0, one launch (start us, length us, event | category | flops | bytes accessed | tf_op | source)
XLA Modules:
  0.0 276.3 jit_solution(5404244537747198390)
XLA Ops:
  7.2 1.4 collective-permute-start.1
  8.6 6.6 %collective-permute-start = (f32[641,2,160]{0,2,1:T(8,128)}, f32[641,2,160]{0,2,1:T(8,128)}, u32[]{:S(2)}, u32[]{:S(2)}) collective-permute-start(f32[641,2,160]{0,2,1:T(8,128)} %bitcast.84), channel_id=1, source_target_pairs={{0,1},{1,2},{2,3},{4,5},{5,6},{6,7},{8,9},{9,10},{10,11},{12,13},{... | collective-permute-start | bytes 2461448 | tf_op jit(solution)/shard_map/ppermute | solution.py:19
  15.2 1.7 copy.28
  17.0 0.6 dynamic_slice.10
  17.6 0.9 slice_reduce_fusion.23
  18.5 1.5 slice_reduce_fusion.24
  20.0 1.3 broadcast_multiply_fusion.3
  21.4 12.9 %collective-permute-done.1 = f32[641,2,160]{0,2,1:T(8,128)S(1)} collective-permute-done((f32[641,2,160]{0,2,1:T(8,128)}, f32[641,2,160]{0,2,1:T(8,128)S(1)}, u32[]{:S(2)}, u32[]{:S(2)}) %collective-permute-start.1) | collective-permute-done | bytes 820512 | tf_op jit(solution)/shard_map/ppermute | solution.py:21
  34.2 1.3 collective-permute-done
  35.5 1.8 pad_maximum_fusion.8
  37.4 2.1 fusion.28
  39.5 3.0 %fusion.29 = (f32[641,6,159]{0,2,1:T(8,128)}, f32[641,6,159]{0,2,1:T(8,128)}) fusion(f32[641,6,160]{0,2,1:T(8,128)S(1)} %pad_maximum_fusion.8), kind=kLoop, calls=%fused_computation.120 | loop fusion | bytes 9784224 | tf_op jit(solution)/shard_map/jit(_roll_static)/slice | solution.py:57
  42.5 4.6 %fusion.3 = (f32[641,6,160]{0,2,1:T(8,128)S(1)}, f32[641,6,160]{0,2,1:T(8,128)S(1)}, f32[641,6,160]{0,2,1:T(8,128)S(1)}, f32[641,6,160]{0,2,1:T(8,128)S(1)}) fusion(f32[641,2,160]{0,2,1:T(8,128)S(1)} %copy-done.13, f32[641,2,160]{0,2,1:T(8,128)S(1)} %bitcast.86, f32[641,2,160]{0,2,1:T(8,128)} %collective-permute-done, ...), kind=kLoop, calls=%fused_computation.10 | loop fusion | flops 7384320 | bytes 22060656 | tf_op jit(solution)/shard_map/jit(_roll_static)/concatenate | solution.py:57
  47.2 5.9 %fusion.27 = (f32[2,160]{1,0:T(2,128)S(1)}, f32[641,2,160]{0,2,1:T(8,128)}) fusion(f32[641,2,160]{0,2,1:T(8,128)S(1)} %bitcast.87, f32[641,6,160]{0,2,1:T(8,128)S(1)} %get-tuple-element.86, f32[641]{0:T(1024)S(1)} %get-tuple-element.72, f32[641]{0:T(1024)S(1)} %get-tuple-element.73, f32[641]{0:T(1024)S(1)} %get-tuple-element.50, ...), kind=kLoop, calls=%fused_computation.118 | loop fusion | flops 10871040 | bytes 19756900 | tf_op jit(solution)/shard_map/reduce_sum | solution.py:82
  53.3 1.5 multiply_reduce_fusion.26
  54.8 0.1 rsqrt.18
  54.8 1.4 fusion.18
  56.3 2.2 multiply_convert_fusion
  58.5 0.4 copy-done.26
  58.8 1.0 fusion.16
  59.9 0.3 convolution_bitcast_fusion.5
  60.2 0.8 copy.26
  60.9 3.9 %all-to-all-start = ((f32[1,72,8,40]{1,3,0,2:T(8,128)}), f32[1,72,8,40]{1,3,0,2:T(8,128)S(1)}, u32[]{:S(2)}, u32[]{:S(2)}) async-start(f32[1,72,8,40]{1,3,0,2:T(8,128)} %bitcast.95), calls=%async_computation | async-start | bytes 327680 | tf_op jit(solution)/shard_map/all_to_all | solution.py:159
  64.9 0.7 dynamic-slice_bitcast_fusion
  65.6 5.1 %all-to-all-done = f32[1,72,8,40]{1,3,0,2:T(8,128)S(1)} async-done(((f32[1,72,8,40]{1,3,0,2:T(8,128)}), f32[1,72,8,40]{1,3,0,2:T(8,128)S(1)}, u32[]{:S(2)}, u32[]{:S(2)}) %all-to-all-start) | async-done | bytes 92192 | tf_op jit(solution)/shard_map/all_to_all | solution.py:159
  70.7 0.8 fusion.14
  71.5 7.5 %all_to_all.30 = bf16[8,72,1,40]{1,3,2,0:T(8,128)(2,1)S(1)} all-to-all(bf16[8,72,1,40]{1,3,2,0:T(8,128)(2,1)S(1)} %fusion.26), channel_id=1, replica_groups=mesh['mem'=8,'lat'=4] {'mem'}, dimensions={0} | all-to-all | bytes 92160 | tf_op jit(solution)/shard_map/all_to_all | solution.py:187
  79.0 1.2 convolution_bitcast_fusion.3
  80.2 1.0 fusion.30
  81.2 3.1 %fusion.19 = f32[1282,641]{0,1:T(8,128)} fusion(bf16[1282,320]{0,1:T(8,128)(2,1)S(1)} %copy-done.21, f32[641,320]{0,1:T(8,128)S(1)} %convolution_bitcast_fusion.3), kind=kOutput, calls=%fused_computation.74 | convolution fusion | flops 526132800 | bytes 4928008 | tf_op jit(solution)/shard_map/dot_general | solution.py:49
  84.3 1.2 fusion.5
  85.5 0.9 copy-done.22
  86.4 3.1 %fusion.22 = f32[641,1282]{1,0:T(8,128)} fusion(bf16[1282,320]{0,1:T(8,128)(2,1)S(1)} %fusion.5, f32[641,320]{0,1:T(8,128)S(1)} %copy-done.18, f32[641]{0:T(1024)S(1)} %copy-done.25), kind=kOutput, calls=%fused_computation.77 | convolution fusion | flops 526337920 | bytes 4930572 | tf_op jit(solution)/shard_map/dot_general | solution.py:49
  89.6 0.6 multiply_reduce_fusion.28
  90.2 2.8 %multiply_reduce_fusion = (f32[641]{0:T(1024)S(1)}, f32[320]{0:T(512)S(1)}, f32[320]{0:T(512)S(1)}, f32[641,320]{0,1:T(8,128)S(1)}) fusion(f32[641,320]{0,1:T(8,128)} %copy-done.17, f32[641]{0:T(1024)S(1)} %copy-done.25, bf16[1282,320]{0,1:T(8,128)(2,1)} %copy-done.22, bf16[641,1282]{1,0:T(8,128)(2,1)S(1)} %copy-done), kind=kOutput, calls=%fused_computation.43 | convolution fusion | flops 527157120 | bytes 4112652 | tf_op jit(solution)/shard_map/dot_general | solution.py:123
  93.0 0.4 fusion.17
  93.5 1.3 copy-done.6
  94.8 0.8 multiply_reduce_fusion.4
  95.6 1.8 copy-done.2
  97.5 0.9 copy-done.4
  98.4 0.2 copy-done.14
  98.6 2.6 multiply_reduce_fusion.1
  101.5 0.2 stack.103
  101.6 42.5 %all-reduce.6 = (f32[]{:T(128)}, f32[25,641]{1,0:T(8,128)}, f32[641]{0:T(1024)}) all-reduce(f32[]{:T(128)} %multiply_reduce_fusion.28, f32[25,641]{1,0:T(8,128)S(1)} %stack.103, f32[641]{0:T(1024)S(1)} %get-tuple-element.26), channel_id=1, replica_groups=mesh['mem'=8,'lat'=4] {'mem','lat'}, use_global_device_ids=true, to_apply=%region_5.6 | all-reduce | flops 16667 | bytes 133336 | tf_op jit(solution)/shard_map/psum | solution.py:175
  144.8 116.7 %all-reduce.5.cloned.1.call-done = (f32[641,1282]{1,0:T(8,128)}, f32[1282,641]{0,1:T(8,128)}, f32[641,72]{0,1:T(8,128)}) async-done(((f32[641,1282]{1,0:T(8,128)}, f32[1282,641]{0,1:T(8,128)}, f32[641,72]{0,1:T(8,128)}), (f32[641,1282]{1,0:T(8,128)}, f32[1282,641]{0,1:T(8,128)}, f32[641,72]{0,1:T(8,128)})) %all-reduce.5.cloned.1.call-update) | async-done | bytes 6758720 | tf_op jit(solution)/shard_map/psum | solution.py:192
  261.5 4.2 %copy.36 = f32[641,1282]{1,0:T(8,128)} copy(f32[641,1282]{1,0:T(8,128)} %get-tuple-element.100) | data formatting | bytes 6574096
  265.8 1.8 copy.37
  267.6 0.7 copy.38
  (88 shorter events, 0.7 us)
Async XLA Ops:
  7.2 49.1 %copy-start = (bf16[641,1282]{1,0:T(8,128)(2,1)S(1)}, bf16[641,1282]{1,0:T(8,128)(2,1)}, u32[]{:S(2)}) copy-start(bf16[641,1282]{1,0:T(8,128)(2,1)} %param.11) | copy-start | bytes 4930576
  7.2 27.1 %collective-permute-start.1 = (f32[641,2,160]{0,2,1:T(8,128)}, f32[641,2,160]{0,2,1:T(8,128)S(1)}, u32[]{:S(2)}, u32[]{:S(2)}) collective-permute-start(f32[641,2,160]{0,2,1:T(8,128)} %bitcast.83), channel_id=1, source_target_pairs={{1,0},{2,1},{3,2},{5,4},{6,5},{7,6},{9,8},{10,9},{11,10},{13,12},{... | collective-permute-start | bytes 2461448 | tf_op jit(solution)/shard_map/ppermute | solution.py:21
  8.6 26.9 %collective-permute-start = (f32[641,2,160]{0,2,1:T(8,128)}, f32[641,2,160]{0,2,1:T(8,128)}, u32[]{:S(2)}, u32[]{:S(2)}) collective-permute-start(f32[641,2,160]{0,2,1:T(8,128)} %bitcast.84), channel_id=1, source_target_pairs={{0,1},{1,2},{2,3},{4,5},{5,6},{6,7},{8,9},{9,10},{10,11},{12,13},{... | collective-permute-start | bytes 2461448 | tf_op jit(solution)/shard_map/ppermute | solution.py:19
  34.2 3.1 %copy-start.12 = (f32[641,2,160]{0,2,1:T(8,128)}, f32[641,2,160]{0,2,1:T(8,128)S(1)}, u32[]{:S(2)}) copy-start(f32[641,2,160]{0,2,1:T(8,128)S(1)} %collective-permute-done.1) | copy-start | bytes 2461444
  39.5 3.0 %copy-start.9 = (f32[1,641,2,160]{1,3,2,0:T(8,128)S(1)}, f32[1,641,2,160]{1,3,2,0:T(8,128)}, u32[]{:S(2)}) copy-start(f32[1,641,2,160]{1,3,2,0:T(8,128)} %param.8) | copy-start | bytes 2461444
  39.5 3.0 %copy-start.13 = (f32[641,2,160]{0,2,1:T(8,128)S(1)}, f32[641,2,160]{0,2,1:T(8,128)}, u32[]{:S(2)}) copy-start(f32[641,2,160]{0,2,1:T(8,128)} %copy-done.12) | copy-start | bytes 2461444
  47.2 6.0 %copy-start.1 = (f32[641,6,160]{0,2,1:T(8,128)}, f32[641,6,160]{0,2,1:T(8,128)S(1)}, u32[]{:S(2)}) copy-start(f32[641,6,160]{0,2,1:T(8,128)S(1)} %get-tuple-element.85) | copy-start | bytes 7384324
  47.2 6.0 %copy-start.3 = (f32[641,6,160]{0,2,1:T(8,128)}, f32[641,6,160]{0,2,1:T(8,128)S(1)}, u32[]{:S(2)}) copy-start(f32[641,6,160]{0,2,1:T(8,128)S(1)} %get-tuple-element.86) | copy-start | bytes 7384324
  47.2 6.0 %copy-start.5 = (f32[641,6,160]{0,2,1:T(8,128)}, f32[641,6,160]{0,2,1:T(8,128)S(1)}, u32[]{:S(2)}) copy-start(f32[641,6,160]{0,2,1:T(8,128)S(1)} %get-tuple-element.84) | copy-start | bytes 7384324
  47.2 6.0 %copy-start.7 = (f32[641,6,160]{0,2,1:T(8,128)}, f32[641,6,160]{0,2,1:T(8,128)S(1)}, u32[]{:S(2)}) copy-start(f32[641,6,160]{0,2,1:T(8,128)S(1)} %get-tuple-element.87) | copy-start | bytes 7384324
  53.2 3.1 %copy-start.25 = (f32[641]{0:T(1024)S(1)}, f32[641]{0:T(1024)}, u32[]{:S(2)}) copy-start(f32[641]{0:T(1024)} %param.10) | copy-start | bytes 7696
  56.2 2.2 copy-start.17
  56.2 2.2 copy-start.10
  56.3 2.6 copy-start.26
  58.5 1.4 copy-start.20
  58.5 1.4 copy-start.23
  60.9 9.7 %all-to-all-start = ((f32[1,72,8,40]{1,3,0,2:T(8,128)}), f32[1,72,8,40]{1,3,0,2:T(8,128)S(1)}, u32[]{:S(2)}, u32[]{:S(2)}) async-start(f32[1,72,8,40]{1,3,0,2:T(8,128)} %bitcast.95), calls=%async_computation | async-start | bytes 327680 | tf_op jit(solution)/shard_map/all_to_all | solution.py:159
  64.8 196.7 %all-reduce.5.cloned.1.call-start = ((), (), s32[]{:S(2)}) async-start(), calls=%async_computation.2 | async-start | bytes 15040512 | tf_op jit(solution)/shard_map/psum | solution.py:192
  70.7 10.5 %copy-start.21 = (bf16[1282,320]{0,1:T(8,128)(2,1)S(1)}, bf16[1282,320]{0,1:T(8,128)(2,1)}, u32[]{:S(2)}) copy-start(bf16[1282,320]{0,1:T(8,128)(2,1)} %copy-done.20) | copy-start | bytes 2461444
  80.2 4.1 %copy-start.15 = (f32[641,320]{0,1:T(8,128)}, f32[641,320]{0,1:T(8,128)S(1)}, u32[]{:S(2)}) copy-start(f32[641,320]{0,1:T(8,128)S(1)} %convolution_bitcast_fusion.3) | copy-start | bytes 2461444
  81.2 3.1 %copy-start.27 = (bf16[1282,641]{0,1:T(8,128)(2,1)S(1)}, bf16[1282,641]{0,1:T(8,128)(2,1)}, u32[]{:S(2)}) copy-start(bf16[1282,641]{0,1:T(8,128)(2,1)} %param.12) | copy-start | bytes 4930576
  81.2 3.1 %copy-start.28 = (f32[1282,320]{0,1:T(8,128)S(1)}, f32[1282,320]{0,1:T(8,128)}, u32[]{:S(2)}) copy-start(f32[1282,320]{0,1:T(8,128)} %get-tuple-element.93) | copy-start | bytes 4922884
  84.3 2.1 copy-start.18
  85.4 0.9 copy-start.22
  89.5 3.5 %copy-start.11 = (f32[641,2,160]{0,2,1:T(8,128)S(1)}, f32[641,2,160]{0,2,1:T(8,128)}, u32[]{:S(2)}) copy-start(f32[641,2,160]{0,2,1:T(8,128)} %get-tuple-element.83) | copy-start | bytes 2461444
  89.5 3.5 %copy-start.16 = (f32[641,320]{0,1:T(8,128)S(1)}, f32[641,320]{0,1:T(8,128)}, u32[]{:S(2)}) copy-start(f32[641,320]{0,1:T(8,128)} %copy-done.15) | copy-start | bytes 2461444
  90.2 3.3 %copy-start.8 = (f32[641,6,160]{0,2,1:T(8,128)S(1)}, f32[641,6,160]{0,2,1:T(8,128)}, u32[]{:S(2)}) copy-start(f32[641,6,160]{0,2,1:T(8,128)} %copy-done.7) | copy-start | bytes 7384324
  93.0 1.8 copy-start.6
  94.8 2.6 copy-start.2
  94.8 3.6 %copy-start.4 = (f32[641,6,160]{0,2,1:T(8,128)S(1)}, f32[641,6,160]{0,2,1:T(8,128)}, u32[]{:S(2)}) copy-start(f32[641,6,160]{0,2,1:T(8,128)} %copy-done.3) | copy-start | bytes 7384324
  94.8 3.8 %copy-start.14 = (f32[641,2,160]{0,2,1:T(8,128)S(1)}, f32[641,2,160]{0,2,1:T(8,128)}, u32[]{:S(2)}) copy-start(f32[641,2,160]{0,2,1:T(8,128)} %copy-done.12) | copy-start | bytes 2461444
  261.5 4.3 %copy-start.19 = (f32[1282,641]{0,1:T(8,128)S(1)}, f32[1282,641]{0,1:T(8,128)}, u32[]{:S(2)}) copy-start(f32[1282,641]{0,1:T(8,128)} %get-tuple-element.101) | copy-start | bytes 9861148
  265.8 1.8 copy-start.24
Sparse Core Ops, SparseCore 0:
  89.6 171.8 all-reduce.4
where the time goes:
time: 277 us; the launch traced here: 276 us
  waiting for transfers between devices  136 us (49%)
  blocking collectives  50 us (18%)
  local copies, waits for them, and re-layouts  24.4 us (9%)
  other arithmetic  21.9 us (8%)
  between operations  16.3 us (6%)
  matrix products  15.7 us (6%)
  starting transfers between devices  11.9 us (4%)
    psum x1, waiting for transfers between devices, local(): lax.psum((grads[0], grads[1], grads[2], grads[3], grads[4]), ('mem', 'lat'))  117 us
    psum x1, blocking collectives, local(): loss = lax.psum(partial_value, ('mem', 'lat')) / member_count  42.5 us
    unnamed x62, local copies, waits for them, and re-layouts  14.2 us
    ppermute x1, waiting for transfers between devices, extended(): lax.ppermute(head, axis, [((i + 1) % count, i) for i in range(ends)])  12.9 us
    all_to_all x1, blocking collectives, local(): lax.all_to_all(cot_rounded, 'mem', split_axis=0, concat_axis=2, tiled=True)  7.49 us
    dot_general x3, matrix products, tail_dot(): lax.dot_general(left, right, (((1,), (1,)), ((), ())), preferred_element_...  7.14 us
    ppermute x1, starting transfers between devices, extended(): lax.ppermute(tail, axis, [(i, (i + 1) % count) for i in range(ends)])  6.55 us
    reduce_sum x1, other arithmetic, forward_apply(): center = summed - jnp.mean(summed, axis=0)  5.94 us
  transfers between devices with their start and end apart: 4, of which 4 were waited for; matrix products, arithmetic and copies ran while one was open for 5% of the time, Pallas kernels for 0%

commit v1 on v0

--- a/solution.py
+++ b/solution.py
@@ -6,6 +6,11 @@
 
 DELTA = 0.1
 EPSILON = 1e-05
+
+
+def step_on_files(here_x):
+    high = lax.psum(here_x, "lat")
+    return lax.psum(high, "mem")
 
 
 def extended(cells, sides, width):
@@ -189,7 +194,7 @@
     grads = backward(
         window, stored_residuals, cotangent, norm_gain, up_weight, down_weight, field_head_weight
     )
-    totals = lax.psum((grads[0], grads[1], grads[2], grads[3], grads[4]), ("mem", "lat"))
+    totals = step_on_files((grads[0], grads[1], grads[2], grads[3], grads[4]))
     return (loss, totals[0], totals[1], totals[2], totals[3], totals[4])
 
 

time: 277 us -> 599 us (2.16)
  waiting for transfers between devices: 136 us -> 454 us
    psum x1 -> x4, waiting for transfers between devices: 117 us -> 435 us  [the longest x2 300 us: step_on_files(): high = lax.psum(here_x, 'lat')]
    unnamed x62 -> x68, local copies, waits for them, and re-layouts: 14.2 us -> 15.9 us
  transfers between devices with their start and end apart: 4 -> 7, of which waited for: 4 -> 7; matrix products, arithmetic and copies ran while one was open for 5% -> 1% of each run, Pallas kernels for 0% -> 0%
where the time goes in v1:
time: 599 us; the launch traced here: 598 us
  waiting for transfers between devices  454 us (76%)
  blocking collectives  46.7 us (8%)
  local copies, waits for them, and re-layouts  29.4 us (5%)
  other arithmetic  22.4 us (4%)
  matrix products  17.3 us (3%)
  between operations  16.1 us (3%)
  starting transfers between devices  12 us (2%)
    psum x2, waiting for transfers between devices, step_on_files(): high = lax.psum(here_x, 'lat')  300 us
    psum x2, waiting for transfers between devices, step_on_files(): return lax.psum(high, 'mem')  135 us
    psum x1, blocking collectives, local(): loss = lax.psum(partial_value, ('mem', 'lat')) / member_count  39.2 us
    unnamed x68, local copies, waits for them, and re-layouts  15.9 us
    ppermute x1, waiting for transfers between devices, extended(): lax.ppermute(head, axis, [((i + 1) % count, i) for i in range(ends)])  12.9 us
  transfers between devices with their start and end apart: 7, of which 7 were waited for; matrix products, arithmetic and copies ran while one was open for 1% of the time, Pallas kernels for 0%

profile of v1, /device:TPU:0, one launch (start us, length us, event | category | flops | bytes accessed | tf_op | source)
XLA Modules:
  0.0 598.2 jit_solution(2550002198743518884)
XLA Ops:
  7.2 1.4 collective-permute-start.1
  8.6 6.6 %collective-permute-start = (f32[641,2,160]{0,2,1:T(8,128)}, f32[641,2,160]{0,2,1:T(8,128)}, u32[]{:S(2)}, u32[]{:S(2)}) collective-permute-start(f32[641,2,160]{0,2,1:T(8,128)} %bitcast.84), channel_id=1, source_target_pairs={{0,1},{1,2},{2,3},{4,5},{5,6},{6,7},{8,9},{9,10},{10,11},{12,13},{... | collective-permute-start | bytes 2461448 | tf_op jit(solution)/shard_map/ppermute | solution.py:24
  15.2 1.7 copy.28
  17.7 0.9 slice_reduce_fusion.23
  18.6 1.5 slice_reduce_fusion.24
  20.0 1.3 broadcast_multiply_fusion.3
  21.3 12.9 %collective-permute-done.1 = f32[641,2,160]{0,2,1:T(8,128)S(1)} collective-permute-done((f32[641,2,160]{0,2,1:T(8,128)}, f32[641,2,160]{0,2,1:T(8,128)S(1)}, u32[]{:S(2)}, u32[]{:S(2)}) %collective-permute-start.1) | collective-permute-done | bytes 820512 | tf_op jit(solution)/shard_map/ppermute | solution.py:26
  34.2 1.3 collective-permute-done
  35.5 1.8 pad_maximum_fusion.8
  37.3 2.1 fusion.28
  39.5 3.0 fusion.29
  42.5 4.6 fusion.3
  47.2 5.9 fusion.27
  53.2 1.5 multiply_reduce_fusion.26
  54.8 1.4 fusion.18
  56.2 2.2 multiply_convert_fusion
  58.8 1.0 fusion.16
  59.8 0.9 convolution_bitcast_fusion.5
  60.7 1.7 copy.26
  62.4 3.9 all-to-all-start
  66.3 0.7 dynamic-slice_bitcast_fusion
  67.1 5.1 all-to-all-done
  72.1 1.4 fusion.14
  73.6 7.5 %all_to_all.30 = bf16[8,72,1,40]{1,3,2,0:T(8,128)(2,1)S(1)} all-to-all(bf16[8,72,1,40]{1,3,2,0:T(8,128)(2,1)S(1)} %fusion.26), channel_id=1, replica_groups=mesh['mem'=8,'lat'=4] {'mem'}, dimensions={0} | all-to-all | bytes 92160 | tf_op jit(solution)/shard_map/all_to_all | solution.py:192
  81.1 1.2 convolution_bitcast_fusion.3
  82.2 3.3 fusion.5
  85.5 1.6 multiply_reduce_fusion
  87.2 3.1 fusion.22
  90.3 3.1 fusion.19
  93.8 1.4 copy-done.6
  95.2 0.8 multiply_reduce_fusion.4
  96.0 1.0 copy-done.2
  97.0 0.9 copy-done.4
  98.1 2.5 multiply_reduce_fusion.1
  100.9 2.6 stack.103
  103.6 1.0 fusion.30
  104.6 33.9 %all-reduce.13.cloned.1.call-done = (f32[25,641]{1,0:T(8,128)}, f32[641]{0:T(1024)}) async-done(((f32[25,641]{1,0:T(8,128)}, f32[641]{0:T(1024)}), (f32[25,641]{1,0:T(8,128)}, f32[641]{0:T(1024)})) %all-reduce.13.cloned.1.call-update) | async-done | bytes 66680 | tf_op jit(solution)/shard_map/psum | solution.py:12
  138.5 266.0 %all-reduce.15.cloned.1.call-done = (f32[641,1282]{1,0:T(8,128)}, f32[1282,641]{0,1:T(8,128)}, f32[641,72]{0,1:T(8,128)}) async-done(((f32[641,1282]{1,0:T(8,128)}, f32[1282,641]{0,1:T(8,128)}, f32[641,72]{0,1:T(8,128)}), (f32[641,1282]{1,0:T(8,128)}, f32[1282,641]{0,1:T(8,128)}, f32[641,72]{0,1:T(8,128)})) %all-reduce.15.cloned.1.call-update) | async-done | bytes 6758720 | tf_op jit(solution)/shard_map/psum | solution.py:12
  404.5 0.7 copy-done.23
  405.3 0.6 multiply_reduce_fusion.28
  406.0 39.2 %psum.77 = f32[]{:T(128)} all-reduce(f32[]{:T(128)} %multiply_reduce_fusion.28), channel_id=1, replica_groups=mesh['mem'=8,'lat'=4] {'mem','lat'}, use_global_device_ids=true, to_apply=%region_5.6 | all-reduce | flops 1 | bytes 8 | tf_op jit(solution)/shard_map/psum | solution.py:180
  445.8 13.0 %all-reduce.9.cloned.1.call-done = (f32[25,641]{1,0:T(8,128)}, f32[641]{0:T(1024)}) async-done(((f32[25,641]{1,0:T(8,128)}, f32[641]{0:T(1024)}), (f32[25,641]{1,0:T(8,128)}, f32[641]{0:T(1024)})) %all-reduce.9.cloned.1.call-update) | async-done | bytes 66680 | tf_op jit(solution)/shard_map/psum | solution.py:13
  458.8 122.1 %all-reduce.11.cloned.1.call-done = (f32[641,1282]{1,0:T(8,128)}, f32[1282,641]{0,1:T(8,128)}, f32[641,72]{0,1:T(8,128)}) async-done(((f32[641,1282]{1,0:T(8,128)}, f32[1282,641]{0,1:T(8,128)}, f32[641,72]{0,1:T(8,128)}), (f32[641,1282]{1,0:T(8,128)}, f32[1282,641]{0,1:T(8,128)}, f32[641,72]{0,1:T(8,128)})) %all-reduce.11.cloned.1.call-update) | async-done | bytes 6758720 | tf_op jit(solution)/shard_map/psum | solution.py:13
  580.9 1.5 copy.40
  582.5 1.3 copy.41
  583.7 4.2 copy.42
  588.0 1.8 copy.43
  589.8 0.7 copy.44
  (103 shorter events, 2.6 us)
Async XLA Ops:
  7.2 49.0 %copy-start = (bf16[641,1282]{1,0:T(8,128)(2,1)S(1)}, bf16[641,1282]{1,0:T(8,128)(2,1)}, u32[]{:S(2)}) copy-start(bf16[641,1282]{1,0:T(8,128)(2,1)} %param.11) | copy-start | bytes 4930576
  7.2 27.1 %collective-permute-start.1 = (f32[641,2,160]{0,2,1:T(8,128)}, f32[641,2,160]{0,2,1:T(8,128)S(1)}, u32[]{:S(2)}, u32[]{:S(2)}) collective-permute-start(f32[641,2,160]{0,2,1:T(8,128)} %bitcast.83), channel_id=1, source_target_pairs={{1,0},{2,1},{3,2},{5,4},{6,5},{7,6},{9,8},{10,9},{11,10},{13,12},{... | collective-permute-start | bytes 2461448 | tf_op jit(solution)/shard_map/ppermute | solution.py:26
  8.6 26.9 %collective-permute-start = (f32[641,2,160]{0,2,1:T(8,128)}, f32[641,2,160]{0,2,1:T(8,128)}, u32[]{:S(2)}, u32[]{:S(2)}) collective-permute-start(f32[641,2,160]{0,2,1:T(8,128)} %bitcast.84), channel_id=1, source_target_pairs={{0,1},{1,2},{2,3},{4,5},{5,6},{6,7},{8,9},{9,10},{10,11},{12,13},{... | collective-permute-start | bytes 2461448 | tf_op jit(solution)/shard_map/ppermute | solution.py:24
  21.3 52.2 %copy-start.28 = (f32[72]{0:T(128)}, f32[72]{0:T(128)S(1)}, u32[]{:S(2)}) copy-start(f32[72]{0:T(128)S(1)} %broadcast_multiply_fusion.3) | copy-start | bytes 868
  34.2 3.1 copy-start.12
  39.5 3.0 copy-start.9
  39.5 3.0 copy-start.13
  47.1 6.0 copy-start.1
  47.1 6.0 copy-start.3
  47.1 6.0 copy-start.5
  47.2 6.0 copy-start.7
  53.1 3.1 copy-start.24
  54.8 1.4 copy-start.26
  56.2 2.2 copy-start.15
  56.2 2.2 copy-start.10
  56.2 2.6 copy-start.30
  58.4 1.4 copy-start.18
  58.4 1.4 copy-start.20
  62.4 9.7 %all-to-all-start = ((f32[1,72,8,40]{1,3,0,2:T(8,128)}), f32[1,72,8,40]{1,3,0,2:T(8,128)S(1)}, u32[]{:S(2)}, u32[]{:S(2)}) async-start(f32[1,72,8,40]{1,3,0,2:T(8,128)} %bitcast.95), calls=%async_computation | async-start | bytes 327680 | tf_op jit(solution)/shard_map/all_to_all | solution.py:164
  66.3 72.2 %all-reduce.13.cloned.1.call-start = ((), (), s32[]{:S(2)}) async-start(), calls=%async_computation.4 | async-start | bytes 204800 | tf_op jit(solution)/shard_map/psum | solution.py:12
  67.1 6.4 %copy-start.22 = (f32[72,40]{0,1:T(8,128)}, f32[72,40]{0,1:T(8,128)S(1)}, u32[]{:S(2)}) copy-start(f32[72,40]{0,1:T(8,128)S(1)} %dynamic-slice_bitcast_fusion) | copy-start | bytes 34564
  82.2 3.3 copy-start.16
  87.2 3.1 copy-start.19
  90.2 3.1 copy-start.11
  90.3 3.1 copy-start.27
  90.3 3.5 copy-start.8
  93.3 1.8 copy-start.6
  95.2 1.8 copy-start.2
  95.2 2.7 copy-start.4
  95.2 2.9 copy-start.14
  103.5 301.0 %all-reduce.15.cloned.1.call-start = ((), (), s32[]{:S(2)}) async-start(), calls=%async_computation.5 | async-start | bytes 15040512 | tf_op jit(solution)/shard_map/psum | solution.py:12
  104.5 354.3 %all-reduce.9.cloned.1.call-start = ((), (), s32[]{:S(2)}) async-start(), calls=%async_computation.2 | async-start | bytes 204800 | tf_op jit(solution)/shard_map/psum | solution.py:13
  138.5 442.4 %all-reduce.11.cloned.1.call-start = ((), (), s32[]{:S(2)}) async-start(), calls=%async_computation.3 | async-start | bytes 15040512 | tf_op jit(solution)/shard_map/psum | solution.py:13
  404.5 0.7 copy-start.23
  404.5 0.8 copy-start.25
  404.5 0.8 copy-start.29
  583.7 4.3 copy-start.17
  588.0 1.8 copy-start.21
Sparse Core Ops, SparseCore 0:
  103.6 34.7 all-reduce.12
  141.6 262.8 all-reduce.14
  407.7 51.0 all-reduce.8
  462.3 118.5 all-reduce.10
